TPU v7x, 32 devices: a whole 2x2x4 slice. The times are simulated.
32 devices in a mesh: re: 4 (over y, x), ka: 8 (over z, core).
Axes of the slice: x: 2, y: 2, z: 4, core: 2. Of those that a mesh axis runs over, the one named last changes fastest.
Arguments:
- lattice_blocks: bfloat16 [192, 2, 3, 256], P(('re', 'ka')), may hold values from -0.4375 to 0.4375
- lattice_coords: int32 [192, 3], P(('re', 'ka')), may hold values from -8 to 8
- kpoint_index: int32 [192, 3], P('ka'), may hold values from 0 to 63
- polarization: float32 [3], replicated, may hold values from -4 to 4
- energy_gap: float32 [192, 32], P('ka'), may hold values from 0.5 to 2.5
- coupling: bfloat16 [8, 96, 2, 32, 8], P('ka', 're'), may hold values from -1 to 1
- phonon_weight: bfloat16 [8, 96], P('ka', 're'), may hold values from 0.19921875 to 5
Outputs:
- rates: float32 [192, 8], P('ka', 're')
All inputs are finite; a program needn't handle non-finite values.
Results may differ from a plain program's by a relative error of at most 0.0014.
Values may be sent and summed in bfloat16 or wider, within the bound.
A program may use at most 128 MiB of HBM per device.

v0:
```python
import math

import jax
import jax.numpy as jnp
from jax import lax
from jax.sharding import PartitionSpec as P

NV = 8
NC = 8
NMODE = 96
NKG = 64


def phase_rows(kpoint_index, coords):
    turns = jnp.mod(jnp.sum(kpoint_index[:, None, :] * coords[None, :, :], axis=2), NKG)
    angle = turns.astype(jnp.float32) * (2.0 * math.pi / NKG)
    cosine = jnp.cos(angle).astype(jnp.bfloat16)
    sine = jnp.sin(angle).astype(jnp.bfloat16)
    count = kpoint_index.shape[0]
    upper = jnp.stack([cosine, -sine], axis=2).reshape(count, -1)
    lower = jnp.stack([sine, cosine], axis=2).reshape(count, -1)
    return jnp.concatenate([upper, lower], axis=0)


def left_factor(momenta, polarization, energy_gap):
    count = momenta.shape[1]
    parts = momenta.reshape(2, count, 3, NV, -1)
    along = (
        parts[:, :, 0] * polarization[0]
        + parts[:, :, 1] * polarization[1]
        + parts[:, :, 2] * polarization[2]
    )
    return (along / energy_gap[None, :, None, :]).astype(jnp.bfloat16).reshape(2, count * NV, -1)


def rate_block(factor, coup, weight):

    def product(left, right):
        return jnp.einsum("qvmj,am->qvja", right, left, preferred_element_type=jnp.float32)

    real_left, imag_left = (factor[0], factor[1])
    real_right, imag_right = (coup[:, :, 0], coup[:, :, 1])
    are = product(real_left, real_right) - product(imag_left, imag_right)
    aim = product(real_left, imag_right) + product(imag_left, real_right)
    power = (are * are + aim * aim) * weight.astype(jnp.float32)[:, :, None, None]
    summed = jnp.sum(power, axis=(1, 2))
    count = factor.shape[1] // NV
    qcount = coup.shape[0]
    return jnp.sum(summed.reshape(qcount, count, NV), axis=2).T * (1.0 / (NMODE * NV * NC))


def body(
    lattice_blocks, lattice_coords, kpoint_index, polarization, energy_gap, coupling, phonon_weight
):
    own_count = kpoint_index.shape[0]
    cols = lattice_blocks.shape[2] * lattice_blocks.shape[3]
    blocks = lax.all_gather(lattice_blocks, "ka", axis=0, tiled=True)
    coords = lax.all_gather(lattice_coords.astype(jnp.bfloat16), "ka", axis=0, tiled=True)
    left = phase_rows(kpoint_index, coords.astype(jnp.int32))
    partial_value = jnp.dot(left, blocks.reshape(-1, cols), preferred_element_type=jnp.float32)
    momenta = lax.psum(partial_value, "re").reshape(2, own_count, cols)
    factor = left_factor(momenta, polarization, energy_gap)
    partial_rates = rate_block(
        factor,
        lax.all_gather(coupling, "ka", axis=0, tiled=True),
        lax.all_gather(phonon_weight, "ka", axis=0, tiled=True),
    )
    return lax.psum_scatter(partial_rates, "re", scatter_dimension=1, tiled=True)


def solution(mesh):
    return jax.shard_map(
        body,
        mesh=mesh,
        in_specs=(
            P(("re", "ka"), None, None, None),
            P(("re", "ka"), None),
            P("ka", None),
            P(),
            P("ka", None),
            P("ka", "re", None, None, None),
            P("ka", "re"),
        ),
        out_specs=P("ka", "re"),
        check_vma=False,
    )
```

profile of v0, /device:TPU:0, one launch (start us, length us, event | category | flops | bytes accessed | tf_op | source)
XLA Modules:
  0.0 103.5 jit_solution(17837021338715821611)
XLA Ops:
  6.5 0.0 all-reduce.3.cloned.1.call-start
  6.5 0.7 convert_bitcast_fusion
  7.2 13.5 %all-gather = bf16[8,6,3]{1,2,0:T(4,128)(2,1)S(1)} all-gather(bf16[1,6,3]{1,2,0:T(4,128)(2,1)S(1)} %convert_bitcast_fusion), channel_id=1, replica_groups=mesh['re'=4,'ka'=8] {'ka'}, dimensions={0}, use_global_device_ids=true | all-gather | bytes 324 | tf_op jit(solution)/shard_map/all_gather | solution.py:58
  20.7 0.1 reshape.103
  20.8 0.8 multiply_reduce_fusion.1
  21.5 0.1 fusion.16
  21.6 0.1 cosine_convert_fusion
  21.7 0.1 copy.53
  21.8 0.1 copy.54
  21.9 14.2 %all_gather.13 = bf16[48,2,3,256]{3,1,2,0:T(2,128)(2,1)S(1)} all-gather(bf16[6,2,3,256]{3,1,2,0:T(2,128)(2,1)} %param.7), channel_id=1, replica_groups=mesh['re'=4,'ka'=8] {'ka'}, dimensions={0}, use_global_device_ids=true | all-gather | bytes 165888 | tf_op jit(solution)/shard_map/all_gather | solution.py:57
  36.1 0.1 copy.55
  36.2 0.0 copy-start
  36.2 0.3 fusion.8
  36.5 0.2 reshape_reshape.3
  36.7 0.0 copy-start.3
  36.7 0.0 copy-start.4
  36.7 0.0 copy-start.2
  36.8 0.0 copy-start.1
  36.8 0.8 copy.56
  37.6 0.0 all-reduce.3.cloned.1.call-update
  37.6 0.0 copy-done
  37.7 16.3 %all_gather.14 = bf16[8,24,2,32,8]{3,1,4,0,2:T(8,128)(2,1)S(1)} all-gather(bf16[1,24,2,32,8]{3,1,4,0,2:T(8,128)(2,1)S(1)} %copy.57), channel_id=1, replica_groups=mesh['re'=4,'ka'=8] {'ka'}, dimensions={0}, use_global_device_ids=true | all-gather | bytes 221184 | tf_op jit(solution)/shard_map/all_gather | solution.py:65
  53.9 0.0 copy-done.3
  53.9 8.7 %all-gather.1 = bf16[8,1,24]{2,1,0:T(2,128)(2,1)S(1)} all-gather(bf16[1,1,24]{2,1,0:T(2,128)(2,1)S(1)} %bitcast.62), channel_id=1, replica_groups=mesh['re'=4,'ka'=8] {'ka'}, dimensions={0}, use_global_device_ids=true | all-gather | bytes 432 | tf_op jit(solution)/shard_map/all_gather | solution.py:66
  62.7 0.0 copy-done.4
  62.7 0.6 dynamic-slice
  63.9 0.0 copy-done.2
  63.9 0.6 fusion.17
  64.6 17.4 %all-reduce.3.cloned.1.call-done = f32[2,24,3,8,32]{4,3,1,0,2:T(8,128)} async-done(((f32[2,24,3,8,32]{4,3,1,0,2:T(8,128)}), f32[2,24,3,8,32]{4,3,1,0,2:T(8,128)}) %all-reduce.3.cloned.1.call-update) | async-done | bytes 147472 | tf_op jit(solution)/shard_map/psum | solution.py:61
  82.0 0.0 copy-done.1
  82.0 3.1 %fusion.7 = bf16[2,24,8,32]{3,2,1,0:T(8,128)(2,1)S(1)} fusion(f32[2,24,3,8,32]{4,3,1,0,2:T(8,128)} %all-reduce.3.cloned.1.call-done, f32[24,32]{1,0:T(8,128)S(1)} %copy-done.1, f32[]{:T(128)} %bitcast.6, f32[]{:T(128)} %bitcast.5, f32[]{:T(128)} %bitcast.4), kind=kLoop, calls=%fused_computation.13 | loop fusion | flops 86016 | bytes 175116 | tf_op jit(solution)/shard_map/convert_element_type | solution.py:33
  85.1 0.4 fusion
  85.5 0.4 fusion.2
  85.9 0.4 fusion.1
  86.3 0.7 multiply_reduce_fusion
  87.0 0.1 reshape.98
  87.1 0.1 reduce_sum.35
  87.2 8.9 %all-reduce = f32[24,8]{0,1:T(8,128)S(1)} all-reduce(f32[24,8]{0,1:T(8,128)S(1)} %multiply_bitcast_fusion), channel_id=2, replica_groups=mesh['re'=4,'ka'=8] {'re'}, use_global_device_ids=true, to_apply=%region_4.5.clone | all-reduce | flops 192 | bytes 1536
  96.1 0.6 constant_dynamic-slice_fusion
  (6 shorter events, 0.1 us)
Async XLA Ops:
  6.5 75.5 %all-reduce.3.cloned.1.call-start = ((), (), s32[]{:S(2)}) async-start(), calls=%async_computation | async-start | bytes 1179648 | tf_op jit(solution)/shard_map/psum | solution.py:61
  36.2 1.4 %copy-start = (bf16[1,24,2,32,8]{3,4,2,1,0:T(8,128)(2,1)S(1)}, bf16[1,24,2,32,8]{3,4,2,1,0:T(8,128)(2,1)}, u32[]{:S(2)}) copy-start(bf16[1,24,2,32,8]{3,4,2,1,0:T(8,128)(2,1)} %param.12) | copy-start | bytes 73732
  36.7 17.2 %copy-start.3 = (bf16[1,24]{1,0:T(2,128)(2,1)S(1)}, bf16[1,24]{1,0:T(2,128)(2,1)}, u32[]{:S(2)}) copy-start(bf16[1,24]{1,0:T(2,128)(2,1)} %param.13) | copy-start | bytes 148
  36.7 25.9 %copy-start.4 = (u32[32]{0:T(128)S(1)}, u32[32]{0:T(128)}, u32[]{:S(2)}) copy-start(u32[32]{0:T(128)} %constant.28) | copy-start | bytes 388
  36.7 27.2 %copy-start.2 = (f32[3]{0:T(128)S(1)}, f32[3]{0:T(128)}, u32[]{:S(2)}) copy-start(f32[3]{0:T(128)} %param.10) | copy-start | bytes 40
  36.8 45.3 %copy-start.1 = (f32[24,32]{1,0:T(8,128)S(1)}, f32[24,32]{1,0:T(8,128)}, u32[]{:S(2)}) copy-start(f32[24,32]{1,0:T(8,128)} %param.11) | copy-start | bytes 9220
Sparse Core Ops, SparseCore 0:
  37.8 44.1 all-reduce.2
where the time goes:
time: 104 us
  blocking collectives  61.6 us (59%)
  waiting for transfers between devices  17.5 us (17%)
  between operations  14.2 us (14%)
  other arithmetic  4.75 us (5%)
  local copies, waits for them, and re-layouts  3.38 us (3%)
  matrix products  2.13 us (2%)
    psum x1, waiting for transfers between devices, body(): momenta = lax.psum(partial_value, 're').reshape(2, own_count, cols)  17.4 us
    all_gather x1, blocking collectives, body(): lax.all_gather(coupling, 'ka', axis=0, tiled=True)  16.3 us
    all_gather x1, blocking collectives, body(): blocks = lax.all_gather(lattice_blocks, 'ka', axis=0, tiled=True)  14.2 us
    all_gather x1, blocking collectives, body(): lax.all_gather(lattice_coords.astype(jnp.bfloat16), 'ka', axis=0, tiled=T...  13.5 us
    unnamed x1, blocking collectives  8.93 us
    all_gather x1, blocking collectives, body(): lax.all_gather(phonon_weight, 'ka', axis=0, tiled=True)  8.72 us
    convert_element_type x1, other arithmetic, left_factor(): (along / energy_gap[None, :, None, :]).astype(jnp.bfloat16)  3.05 us
  transfers between devices with their start and end apart: 1, of which 1 were waited for; matrix products, arithmetic and copies ran while one was open for 1% of the time, Pallas kernels for 0%

commit v1 on v0

v1 whole, which is shorter than its diff:
```python
import functools
import math

import jax
import jax.numpy as jnp
from jax import lax
from jax.experimental import pallas as pl
from jax.experimental.pallas import tpu as pltpu
from jax.sharding import PartitionSpec as P

NKG = 64
NC_LANES = 128
MESH = pl.DeviceIdType.MESH
F32, BF16 = jnp.float32, jnp.bfloat16


def iota(shape, axis):
    return lax.broadcasted_iota(jnp.int32, shape, axis)


def each(n, f):
    if n <= 8:
        for i in range(1, n):
            f(i)
    else:
        pl.loop(1, n)(f)


def kernel(
    dims, pol, blk, coords, kidx, gap, coup, weight, out,
    stage, gath, coups, part, rate,
    w_send, w_recv, c_send, c_recv, p_send, p_recv, r_send, r_recv,
):
    ren, kan = dims
    re, ka = lax.axis_index("re"), lax.axis_index("ka")
    own_r = blk.shape[0]
    cols = blk.shape[3]
    half = stage.shape[0]
    group = NC_LANES // half
    count = kidx.shape[1]
    nb = gap.shape[1]
    nv = cols // nb
    modes, nc = coup.shape[1], coup.shape[3]
    mh = modes // 2
    rows = mh * nc
    q_own = coup.shape[0]
    qn = kan * q_own
    kv = nv * count

    barrier = pltpu.get_barrier_semaphore()

    def peer(n, me, i):
        return lax.rem(me + i, n)

    def hello_ka(i):
        pl.semaphore_signal(barrier, inc=1, device_id={"ka": peer(kan, ka, i)}, device_id_type=MESH)

    def hello_re(i):
        pl.semaphore_signal(barrier, inc=1, device_id={"re": peer(ren, re, i)}, device_id_type=MESH)

    each(kan, hello_ka)
    each(ren, hello_re)

    stage[...] = jnp.zeros_like(stage)
    for r in range(own_r):
        stage[2 * r : 2 * r + 2, :] = (
            blk[r, 0].astype(F32) * pol[0] + blk[r, 1].astype(F32) * pol[1] + blk[r, 2].astype(F32) * pol[2]
        )
    base = lax.rem(ka, group) * half
    spot = iota((own_r, NC_LANES), 1) - base - 2 * iota((own_r, NC_LANES), 0)
    spread = jnp.where((spot == 0) | (spot == 1), 1.0, 0.0).astype(BF16)
    stage[2 * own_r : 2 * own_r + 3, 0:NC_LANES] = jnp.dot(
        coords[...].astype(F32).astype(BF16), spread, preferred_element_type=F32
    )
    whole = stage[...]
    high = whole.astype(BF16)
    gath[ka, 0:half, :] = high
    gath[ka, half:, :] = (whole - high.astype(F32)).astype(BF16)

    for q in range(q_own):
        pieces = [
            coup[q, h * mh : (h + 1) * mh, part_of].astype(F32).reshape(rows, nb)
            for h in range(2)
            for part_of in range(2)
        ]
        coups[ka * q_own + q, 0:rows, :] = jnp.concatenate(pieces, axis=1).astype(BF16)
        wide = jnp.broadcast_to(weight[q : q + 1, :].astype(F32), (16, modes))
        line, lane = iota((16, modes), 0), iota((16, modes), 1)
        w0 = jnp.sum(jnp.where((lane == line) & (line < mh), wide, 0.0), axis=1, keepdims=True)
        w1 = jnp.sum(jnp.where((lane == line + mh) & (line < mh), wide, 0.0), axis=1, keepdims=True)
        coups[ka * q_own + q, rows:, :] = jnp.where(
            iota((16, NC_LANES), 1) < NC_LANES // 2, w0, w1
        ).astype(BF16)

    pl.semaphore_wait(barrier, kan - 1 + ren - 1)

    def w_copy(i):
        return pltpu.make_async_remote_copy(
            gath.at[ka], gath.at[ka], w_send.at[i], w_recv.at[ka],
            device_id={"ka": peer(kan, ka, i)}, device_id_type=MESH,
        )

    def c_copy(i):
        mine = coups.at[pl.ds(ka * q_own, q_own)]
        return pltpu.make_async_remote_copy(
            mine, mine, c_send.at[i], c_recv.at[ka],
            device_id={"ka": peer(kan, ka, i)}, device_id_type=MESH,
        )

    each(kan, lambda i: w_copy(i).start())
    each(kan, lambda i: c_copy(i).start())

    square = iota((count, count), 0) == iota((count, count), 1)
    kcols = [
        jnp.sum(jnp.where(square, jnp.broadcast_to(kidx[d : d + 1, :].astype(F32), (count, count)), 0.0),
                axis=1, keepdims=True)
        for d in range(3)
    ]

    def w_wait(i):
        slot = peer(kan, ka, i)
        pltpu.make_async_remote_copy(
            gath.at[slot], gath.at[slot], w_send.at[i], w_recv.at[slot],
            device_id={"ka": slot}, device_id_type=MESH,
        ).wait_recv()

    each(kan, w_wait)

    lanes = iota((count, group * half), 1)
    inside = lax.rem(lanes, half)
    used = inside < 2 * own_r
    even = lax.rem(lanes, 2) == 0

    def partial_of(g):
        block = gath[pl.ds(g * group, group)]
        where = block[:, 0:half, 0:NC_LANES].astype(F32)
        here = jnp.sum(where, axis=0)[2 * own_r : 2 * own_r + 3]
        turns = kcols[0] * here[0:1] + kcols[1] * here[1:2] + kcols[2] * here[2:3]
        turns = turns - NKG * jnp.floor(turns * (1.0 / NKG))
        angle = turns * (2.0 * math.pi / NKG)
        cosine = jnp.where(used, jnp.cos(angle), 0.0)
        sine = jnp.where(used, jnp.sin(angle), 0.0)
        left = jnp.concatenate(
            [jnp.where(even, cosine, -sine), jnp.where(even, sine, cosine)], axis=0
        ).astype(BF16)
        return jnp.dot(
            left, block[:, 0:half].reshape(group * half, cols), preferred_element_type=F32
        ) + jnp.dot(left, block[:, half:].reshape(group * half, cols), preferred_element_type=F32)

    if kan == group:
        part[re] = partial_of(0)
    else:
        part[re] = partial_of(0)

        @pl.loop(1, kan // group)
        def _(g):
            part[re] += partial_of(g)

    def p_copy(i):
        return pltpu.make_async_remote_copy(
            part.at[re], part.at[re], p_send.at[i], p_recv.at[re],
            device_id={"re": peer(ren, re, i)}, device_id_type=MESH,
        )

    each(ren, lambda i: p_copy(i).start())

    gaps = jnp.concatenate([gap[...]] * nv, axis=1)
    kv2 = 2 * kv
    pick = jnp.where(
        lax.rem(iota((kv2, NC_LANES), 0), count) == iota((kv2, NC_LANES), 1), 1.0, 0.0
    ).astype(BF16)

    def p_wait(i):
        slot = peer(ren, re, i)
        pltpu.make_async_remote_copy(
            part.at[slot], part.at[slot], p_send.at[i], p_recv.at[slot],
            device_id={"re": slot}, device_id_type=MESH,
        ).wait_recv()

    each(ren, p_wait)
    total = part[0]
    for i in range(1, ren):
        total = total + part[i]
    real = total[0:count] / gaps
    imag = total[count:] / gaps
    per = NC_LANES // nb
    lane = iota((count, NC_LANES), 1)

    def rolled(x):
        tiles = [x[:, t * NC_LANES : (t + 1) * NC_LANES] for t in range(cols // NC_LANES)]
        return [[pltpu.roll(t, nb * s, 1) if s else t for s in range(per)] for t in tiles]

    reals, imags = rolled(real), rolled(imag)

    def rows_of(first, second, sign, h):
        blocks = []
        for v in range(nv):
            a = first[v // per][(2 * h - v) % per]
            b = second[v // per][(2 * h + 1 - v) % per]
            start = 2 * h * nb
            x = jnp.where(lane < start + nb, a, sign * b)
            blocks.append(jnp.where((lane >= start) & (lane < start + 2 * nb), x, 0.0))
        return blocks

    left = jnp.concatenate(
        rows_of(reals, imags, -1.0, 0) + rows_of(reals, imags, -1.0, 1)
        + rows_of(imags, reals, 1.0, 0) + rows_of(imags, reals, 1.0, 1),
        axis=0,
    ).astype(BF16)

    def c_wait(i):
        slot = peer(kan, ka, i)
        there = coups.at[pl.ds(slot * q_own, q_own)]
        pltpu.make_async_remote_copy(
            there, there, c_send.at[i], c_recv.at[slot],
            device_id={"ka": slot}, device_id_type=MESH,
        ).wait_recv()

    each(kan, c_wait)
    many = math.gcd(qn, 8)

    def rates_of(g):
        held = coups[pl.ds(g * many, many)]
        amp = lax.dot_general(
            held[:, 0:rows].reshape(many * rows, NC_LANES), left,
            (((1,), (1,)), ((), ())), preferred_element_type=F32,
        )
        lines = []
        for q in range(many):
            w = held[q, rows:].astype(F32)
            w_lanes = jnp.concatenate(
                [jnp.broadcast_to(w[:, 0:1], (16, kv)), jnp.broadcast_to(w[:, NC_LANES - 1 :], (16, kv))], axis=1
            )
            acc = None
            for i in range(mh):
                at = q * rows + i * nc
                a, b = amp[at : at + nc, 0:kv2], amp[at : at + nc, kv2:]
                term = (a * a + b * b) * w_lanes[i : i + 1]
                acc = term if acc is None else acc + term
            lines.append(jnp.sum(acc, axis=0, keepdims=True))
        flat = jnp.concatenate(lines, axis=0)
        got = None
        for _ in range(3):
            head = flat.astype(BF16)
            flat = flat - head.astype(F32)
            piece = jnp.dot(head, pick, preferred_element_type=F32)
            got = piece if got is None else got + piece
        rate[re, pl.ds(pl.multiple_of(g * many, many), many), :] = got

    if qn == many:
        rates_of(0)
    else:
        pl.loop(0, qn // many)(rates_of)

    def r_copy(i):
        return pltpu.make_async_remote_copy(
            rate.at[re], rate.at[re], r_send.at[i], r_recv.at[re],
            device_id={"re": peer(ren, re, i)}, device_id_type=MESH,
        )

    each(ren, lambda i: r_copy(i).start())

    def r_wait(i):
        slot = peer(ren, re, i)
        pltpu.make_async_remote_copy(
            rate.at[slot], rate.at[slot], r_send.at[i], r_recv.at[slot],
            device_id={"re": slot}, device_id_type=MESH,
        ).wait_recv()

    each(kan, lambda i: w_copy(i).wait_send())
    each(kan, lambda i: c_copy(i).wait_send())
    each(ren, lambda i: p_copy(i).wait_send())
    each(ren, r_wait)
    q_out = out.shape[0]
    mine = pl.ds(re * q_out, q_out)
    summed = rate[0, mine, :]
    for i in range(1, ren):
        summed = summed + rate[i, mine, :]
    out[...] = summed[:, 0:count] * (1.0 / (modes * ren * nv * nc))
    each(ren, lambda i: r_copy(i).wait_send())


def body(dims, lattice_blocks, lattice_coords, kpoint_index, polarization, energy_gap, coupling, phonon_weight):
    ren, kan = dims
    own_r, _, _, cols = lattice_blocks.shape
    count = kpoint_index.shape[0]
    q_own, modes, _, _, nc = coupling.shape
    rows = modes // 2 * nc
    half = 16 * pl.cdiv(2 * own_r + 3, 16)
    qn = q_own * kan
    vmem = pl.BlockSpec(memory_space=pltpu.VMEM)
    dma = pltpu.SemaphoreType.DMA
    rates = pl.pallas_call(
        functools.partial(kernel, dims),
        out_shape=jax.ShapeDtypeStruct((qn // ren, count), F32),
        in_specs=[pl.BlockSpec(memory_space=pltpu.SMEM)] + [vmem] * 6,
        out_specs=vmem,
        scratch_shapes=[
            pltpu.VMEM((half, cols), F32),
            pltpu.VMEM((kan, 2 * half, cols), BF16),
            pltpu.VMEM((qn, rows + 16, NC_LANES), BF16),
            pltpu.VMEM((ren, 2 * count, cols), F32),
            pltpu.VMEM((ren, qn, NC_LANES), F32),
            dma((kan,)), dma((kan,)), dma((kan,)), dma((kan,)),
            dma((ren,)), dma((ren,)), dma((ren,)), dma((ren,)),
        ],
        compiler_params=pltpu.CompilerParams(collective_id=0, has_side_effects=True),
    )(
        polarization,
        lattice_blocks.transpose(0, 2, 1, 3),
        lattice_coords.T,
        kpoint_index.T,
        energy_gap,
        coupling.transpose(0, 1, 2, 4, 3),
        phonon_weight,
    )
    return rates.T


def solution(mesh):
    dims = (mesh.shape["re"], mesh.shape["ka"])
    return jax.shard_map(
        functools.partial(body, dims),
        mesh=mesh,
        in_specs=(
            P(("re", "ka"), None, None, None),
            P(("re", "ka"), None),
            P("ka", None),
            P(),
            P("ka", None),
            P("ka", "re", None, None, None),
            P("ka", "re"),
        ),
        out_specs=P("ka", "re"),
        check_vma=False,
    )
```

time: 104 us -> 23 us (0.22)
  blocking collectives: 61.6 us -> 0 us
  Pallas kernels: 0 us -> 21.7 us
  waiting for transfers between devices: 17.5 us -> 0 us
  between operations: 14.2 us -> 0.02 us
  other arithmetic: 4.75 us -> 0 us
  local copies, waits for them, and re-layouts: 3.38 us -> 1.21 us
  matrix products: 2.13 us -> 0 us
    all_gather x4 -> x0, blocking collectives: 52.7 us -> none  [the longest x1 16.3 us: body(): lax.all_gather(coupling, 'ka', axis=0, tiled=True)]
    pallas_call x0 -> x1, Pallas kernels: none -> 21.7 us  [body(): pl.pallas_call(functools.partial(kernel, dims), out_shape=jax.ShapeDtypeS...]
    psum x1 -> x0, waiting for transfers between devices: 17.4 us -> none  [body(): momenta = lax.psum(partial_value, 're').reshape(2, own_count, cols)]
    unnamed x1 -> x0, blocking collectives: 8.93 us -> none
    convert_element_type x4 -> x0, other arithmetic: 3.13 us -> none  [the longest x1 3.05 us: left_factor(): (along / energy_gap[None, :, None, :]).astype(jnp.bfloat16)]
    dot_general x5 -> x0, matrix products: 2.13 us -> none  [the longest x4 1.87 us: product(): jnp.einsum('qvmj,am->qvja', right, left, preferred_element_type=jnp.float32)]
    another operation x4 -> x0, local copies, waits for them, and re-layouts: 1.26 us -> none  [the longest x2 1.06 us: left_factor(): parts = momenta.reshape(2, count, 3, NV, -1)]
  transfers between devices with their start and end apart: 1 -> 0, of which waited for: 1 -> 0; matrix products, arithmetic and copies ran while one was open for 1% -> 0% of each run, Pallas kernels for 0% -> 0%
where the time goes in v1:
time: 23 us; the launch traced here: 22.9 us
  Pallas kernels  21.7 us (94%)
  local copies, waits for them, and re-layouts  1.21 us (5%)
    pallas_call x1, Pallas kernels, body(): pl.pallas_call(functools.partial(kernel, dims), out_shape=jax.ShapeDtypeS...  21.7 us
    unnamed x3, local copies, waits for them, and re-layouts  1.21 us

profile of v1, /device:TPU:0, one launch (start us, length us, event | category | flops | bytes accessed | tf_op | source)
XLA Modules:
  0.0 22.9 jit_solution(13090821027573207583)
XLA Ops:
  0.0 21.7 %shard_map.73 = f32[2,24]{1,0:T(2,128)} custom-call(f32[3]{0:T(128)} %pol.1, bf16[6,3,2,256]{3,2,1,0:T(2,128)(2,1)} %bitcast.6, s32[3,6]{1,0:T(4,128)} %bitcast.8, s32[3,24]{1,0:T(4,128)} %bitcast.9, f32[24,32]{1,0:T(8,128)} %gap.1, bf16[1,24,2,8,32]{4,3,2,1,0:T(8,128)(2,1)} %bitcast.5, bf16[1,24]{1,0:T(2,128)(2,1)} %weight.1), custom_call_target="tpu_custom_call" | custom-call | tf_op jit(solution)/shard_map/pallas_call | solution.py:293
  21.7 0.0 copy-start
  21.7 0.7 %copy-done = f32[2,24]{1,0:T(2,128)S(1)} copy-done((f32[2,24]{1,0:T(2,128)S(1)}, f32[2,24]{1,0:T(2,128)}, u32[]{:S(2)}) %copy-start) | copy-done | bytes 216
  22.3 0.6 %copy.9 = f32[24,2]{0,1:T(2,128)} copy(f32[24,2]{0,1:T(2,128)S(1)} %bitcast.7) | data formatting | bytes 384
Async XLA Ops:
  21.7 0.7 %copy-start = (f32[2,24]{1,0:T(2,128)S(1)}, f32[2,24]{1,0:T(2,128)}, u32[]{:S(2)}) copy-start(f32[2,24]{1,0:T(2,128)} %shard_map.73) | copy-start | bytes 580

commit v2 on v1

v2 whole, which is shorter than its diff:
```python
import functools
import math

import jax
import jax.numpy as jnp
from jax import lax
from jax.experimental import pallas as pl
from jax.experimental.pallas import tpu as pltpu
from jax.sharding import PartitionSpec as P

NKG = 64
NC_LANES = 128
MESH = pl.DeviceIdType.MESH
F32, BF16 = jnp.float32, jnp.bfloat16


def iota(shape, axis):
    return lax.broadcasted_iota(jnp.int32, shape, axis)


def each(n, f):
    if n <= 8:
        for i in range(1, n):
            f(i)
    else:
        pl.loop(1, n)(f)


def kernel(
    dims, pol, blk, coords, kidx, gap, coup, weight, out,
    stage, gath, gpart, gall, part,
    w_send, w_recv, g_send, g_recv, b_send, b_recv, p_send, p_recv,
):
    ren, kan = dims
    re, ka = lax.axis_index("re"), lax.axis_index("ka")
    own_r = blk.shape[0]
    cols = blk.shape[3]
    half = stage.shape[0]
    group = NC_LANES // half
    count = kidx.shape[1]
    nb = gap.shape[1]
    nv = cols // nb
    modes, nc = coup.shape[1], coup.shape[3]
    rows = modes * nc
    q_own = coup.shape[0]
    q_out = out.shape[0]
    tall = nb // 2
    owner = (ka * q_own) // q_out
    spot_out = lax.rem(ka * q_own, q_out)

    barrier = pltpu.get_barrier_semaphore()

    def peer(n, me, i):
        return lax.rem(me + i, n)

    def hello_ka(i):
        pl.semaphore_signal(barrier, inc=1, device_id={"ka": peer(kan, ka, i)}, device_id_type=MESH)

    def hello_re(i):
        pl.semaphore_signal(barrier, inc=1, device_id={"re": peer(ren, re, i)}, device_id_type=MESH)

    each(kan, hello_ka)
    each(ren, hello_re)

    stage[...] = jnp.zeros_like(stage)
    for r in range(own_r):
        stage[2 * r : 2 * r + 2, :] = (
            blk[r, 0].astype(F32) * pol[0] + blk[r, 1].astype(F32) * pol[1] + blk[r, 2].astype(F32) * pol[2]
        )
    base = lax.rem(ka, group) * half
    spot = iota((own_r, NC_LANES), 1) - base - 2 * iota((own_r, NC_LANES), 0)
    spread = jnp.where((spot == 0) | (spot == 1), 1.0, 0.0).astype(BF16)
    stage[2 * own_r : 2 * own_r + 3, 0:NC_LANES] = jnp.dot(
        coords[...].astype(F32).astype(BF16), spread, preferred_element_type=F32
    )
    whole = stage[...]
    high = whole.astype(BF16)
    gath[ka, 0:half, :] = high
    gath[ka, half:, :] = (whole - high.astype(F32)).astype(BF16)

    for q in range(q_own):
        flat = jnp.concatenate(
            [coup[q, :, part_of].astype(F32).reshape(rows, nb) for part_of in range(2)], axis=1
        )
        wide = jnp.broadcast_to(weight[q : q + 1, :].astype(F32), (rows, modes))
        at_mode = iota((rows, modes), 1) == iota((rows, modes), 0) // nc
        scaled = flat * jnp.sum(jnp.where(at_mode, wide, 0.0), axis=1, keepdims=True)
        top = scaled.astype(BF16)
        low = (scaled - top.astype(F32)).astype(BF16)
        flat = flat.astype(BF16)
        gram = sum(
            lax.dot_general(x, flat, (((0,), (0,)), ((), ())), preferred_element_type=F32) for x in (top, low)
        )
        same = gram[0:nb, 0:nb] + gram[nb:, nb:]
        cross = gram[nb:, 0:nb] - gram[0:nb, nb:]
        gpart[re, q * tall : (q + 1) * tall, :] = jnp.concatenate(
            [same[0:tall], cross[0:tall], same[tall:], cross[tall:]], axis=1
        )

    pl.semaphore_wait(barrier, kan - 1 + ren - 1)

    def w_copy(i):
        return pltpu.make_async_remote_copy(
            gath.at[ka], gath.at[ka], w_send.at[i], w_recv.at[ka],
            device_id={"ka": peer(kan, ka, i)}, device_id_type=MESH,
        )

    def g_copy():
        return pltpu.make_async_remote_copy(
            gpart.at[re], gpart.at[re], g_send.at[0], g_recv.at[re],
            device_id={"re": owner}, device_id_type=MESH,
        )

    def b_copy(i):
        mine = gall.at[pl.ds(spot_out, q_own)]
        return pltpu.make_async_remote_copy(
            mine, mine, b_send.at[i], b_recv.at[spot_out // q_own],
            device_id={"ka": peer(kan, ka, i)}, device_id_type=MESH,
        )

    each(kan, lambda i: w_copy(i).start())

    @pl.when(re != owner)
    def _():
        g_copy().start()


    square = iota((count, count), 0) == iota((count, count), 1)
    kcols = [
        jnp.sum(jnp.where(square, jnp.broadcast_to(kidx[d : d + 1, :].astype(F32), (count, count)), 0.0),
                axis=1, keepdims=True)
        for d in range(3)
    ]

    @pl.when(re == owner)
    def _():
        def g_wait(i):
            slot = peer(ren, re, i)
            pltpu.make_async_remote_copy(
                gpart.at[slot], gpart.at[slot], g_send.at[0], g_recv.at[slot],
                device_id={"re": slot}, device_id_type=MESH,
            ).wait_recv()

        each(ren, g_wait)
        gram = gpart[0]
        for i in range(1, ren):
            gram = gram + gpart[i]
        for q in range(q_own):
            gall[spot_out + q] = gram[q * tall : (q + 1) * tall]
        each(kan, lambda i: b_copy(i).start())

    def w_wait(i):
        slot = peer(kan, ka, i)
        pltpu.make_async_remote_copy(
            gath.at[slot], gath.at[slot], w_send.at[i], w_recv.at[slot],
            device_id={"ka": slot}, device_id_type=MESH,
        ).wait_recv()

    each(kan, w_wait)

    lanes = iota((count, group * half), 1)
    inside = lax.rem(lanes, half)
    used = inside < 2 * own_r
    even = lax.rem(lanes, 2) == 0

    def partial_of(g):
        block = gath[pl.ds(g * group, group)]
        where = block[:, 0:half, 0:NC_LANES].astype(F32)
        here = jnp.sum(where, axis=0)[2 * own_r : 2 * own_r + 3]
        turns = kcols[0] * here[0:1] + kcols[1] * here[1:2] + kcols[2] * here[2:3]
        turns = turns - NKG * jnp.floor(turns * (1.0 / NKG))
        angle = turns * (2.0 * math.pi / NKG)
        cosine = jnp.where(used, jnp.cos(angle), 0.0)
        sine = jnp.where(used, jnp.sin(angle), 0.0)
        left = jnp.concatenate(
            [jnp.where(even, cosine, -sine), jnp.where(even, sine, cosine)], axis=0
        ).astype(BF16)
        return jnp.dot(
            left, block[:, 0:half].reshape(group * half, cols), preferred_element_type=F32
        ) + jnp.dot(left, block[:, half:].reshape(group * half, cols), preferred_element_type=F32)

    if kan == group:
        part[re] = partial_of(0)
    else:
        part[re] = partial_of(0)

        @pl.loop(1, kan // group)
        def _(g):
            part[re] += partial_of(g)

    def p_copy(i):
        return pltpu.make_async_remote_copy(
            part.at[re], part.at[re], p_send.at[i], p_recv.at[re],
            device_id={"re": peer(ren, re, i)}, device_id_type=MESH,
        )

    each(ren, lambda i: p_copy(i).start())

    gaps = jnp.concatenate([gap[...]] * nv, axis=1)
    def p_wait(i):
        slot = peer(ren, re, i)
        pltpu.make_async_remote_copy(
            part.at[slot], part.at[slot], p_send.at[i], p_recv.at[slot],
            device_id={"re": slot}, device_id_type=MESH,
        ).wait_recv()

    each(ren, p_wait)
    total = part[0]
    for i in range(1, ren):
        total = total + part[i]
    real = total[0:count] / gaps
    imag = total[count:] / gaps
    per = NC_LANES // nb
    quarter = iota((count, NC_LANES), 1) // nb

    def rolled(x):
        x = x.astype(BF16).astype(F32)
        tiles = [x[:, t * NC_LANES : (t + 1) * NC_LANES] for t in range(cols // NC_LANES)]
        return [[pltpu.roll(t, nb * s, 1) if s else t for s in range(per)] for t in tiles]

    reals, imags = rolled(real), rolled(imag)
    blocks = []
    for v in range(nv):
        x = imags[v // per][(3 - v) % per]
        x = jnp.where(quarter == 2, reals[v // per][(2 - v) % per], x)
        x = jnp.where(quarter == 1, imags[v // per][(1 - v) % per], x)
        blocks.append(jnp.where(quarter == 0, reals[v // per][(0 - v) % per], x))
    left = jnp.concatenate(blocks, axis=0)
    left16 = left.astype(BF16)

    first = (re * q_out) // q_own
    for step in range(q_out // q_own):

        @pl.when(first + step != ka)
        def _():
            there = gall.at[pl.ds(step * q_own, q_own)]
            pltpu.make_async_remote_copy(
                there, there, b_send.at[0], b_recv.at[step],
                device_id={"ka": first + step}, device_id_type=MESH,
            ).wait_recv()

    def square_of(packed):
        a, b = packed[:, 0 : 2 * nb], packed[:, 2 * nb :]
        rows_of = jnp.concatenate([a, b], axis=0)
        same, cross = rows_of[:, 0:nb], rows_of[:, nb:]
        return jnp.concatenate(
            [rows_of, jnp.concatenate([-cross, same], axis=1)], axis=0
        )

    scale = 1.0 / (modes * ren * nv * nc)
    choose = jnp.where(iota((8, NC_LANES), 1) // (2 * nb) == iota((8, NC_LANES), 0), 1.0, 0.0).astype(BF16)
    for pair in range(q_out // 2):
        right = jnp.concatenate([square_of(gall[2 * pair]), square_of(gall[2 * pair + 1])], axis=1)
        top = right.astype(BF16)
        low = (right - top.astype(F32)).astype(BF16)
        power = left * jnp.dot(
            left16, jnp.concatenate([top, low], axis=0), preferred_element_type=F32
        )
        summed = power[0:count]
        for v in range(1, nv):
            summed = summed + power[v * count : (v + 1) * count]
        got = None
        for _ in range(3):
            head = summed.astype(BF16)
            summed = summed - head.astype(F32)
            piece = lax.dot_general(choose, head, (((1,), (1,)), ((), ())), preferred_element_type=F32)
            got = piece if got is None else got + piece
        out[2 * pair : 2 * pair + 2, :] = got[0:2] * scale

    each(kan, lambda i: w_copy(i).wait_send())
    each(ren, lambda i: p_copy(i).wait_send())

    @pl.when(re != owner)
    def _():
        g_copy().wait_send()

    @pl.when(re == owner)
    def _():
        each(kan, lambda i: b_copy(i).wait_send())


def body(dims, lattice_blocks, lattice_coords, kpoint_index, polarization, energy_gap, coupling, phonon_weight):
    ren, kan = dims
    own_r, _, _, cols = lattice_blocks.shape
    count = kpoint_index.shape[0]
    q_own = coupling.shape[0]
    tall = energy_gap.shape[1] // 2
    half = 16 * pl.cdiv(2 * own_r + 3, 16)
    q_out = q_own * kan // ren
    vmem = pl.BlockSpec(memory_space=pltpu.VMEM)
    dma = pltpu.SemaphoreType.DMA
    rates = pl.pallas_call(
        functools.partial(kernel, dims),
        out_shape=jax.ShapeDtypeStruct((q_out, count), F32),
        in_specs=[pl.BlockSpec(memory_space=pltpu.SMEM)] + [vmem] * 6,
        out_specs=vmem,
        scratch_shapes=[
            pltpu.VMEM((half, cols), F32),
            pltpu.VMEM((kan, 2 * half, cols), BF16),
            pltpu.VMEM((ren, q_own * tall, NC_LANES), F32),
            pltpu.VMEM((q_out, tall, NC_LANES), F32),
            pltpu.VMEM((ren, 2 * count, cols), F32),
            dma((kan,)), dma((kan,)), dma((1,)), dma((ren,)),
            dma((kan,)), dma((q_out // q_own,)), dma((ren,)), dma((ren,)),
        ],
        compiler_params=pltpu.CompilerParams(collective_id=0, has_side_effects=True),
    )(
        polarization,
        lattice_blocks.transpose(0, 2, 1, 3),
        lattice_coords.T,
        kpoint_index.T,
        energy_gap,
        coupling.transpose(0, 1, 2, 4, 3),
        phonon_weight,
    )
    return rates.T


def solution(mesh):
    dims = (mesh.shape["re"], mesh.shape["ka"])
    return jax.shard_map(
        functools.partial(body, dims),
        mesh=mesh,
        in_specs=(
            P(("re", "ka"), None, None, None),
            P(("re", "ka"), None),
            P("ka", None),
            P(),
            P("ka", None),
            P("ka", "re", None, None, None),
            P("ka", "re"),
        ),
        out_specs=P("ka", "re"),
        check_vma=False,
    )
```

time: 23 us -> 17.6 us (0.77)
  Pallas kernels: 21.7 us -> 16.3 us
    pallas_call x1, Pallas kernels: 21.7 us -> 16.3 us  [body(): pl.pallas_call(functools.partial(kernel, dims), out_shape=jax.ShapeDtypeS...]
where the time goes in v2:
time: 17.6 us; the launch traced here: 17.5 us
  Pallas kernels  16.3 us (93%)
  local copies, waits for them, and re-layouts  1.21 us (7%)
    pallas_call x1, Pallas kernels, body(): pl.pallas_call(functools.partial(kernel, dims), out_shape=jax.ShapeDtypeS...  16.3 us
    unnamed x3, local copies, waits for them, and re-layouts  1.21 us

profile of v2, /device:TPU:0, one launch (start us, length us, event | category | flops | bytes accessed | tf_op | source)
XLA Modules:
  0.0 17.5 jit_solution(15773191656476603405)
XLA Ops:
  0.0 16.3 %shard_map.73 = f32[2,24]{1,0:T(2,128)} custom-call(f32[3]{0:T(128)} %pol.1, bf16[6,3,2,256]{3,2,1,0:T(2,128)(2,1)} %bitcast.6, s32[3,6]{1,0:T(4,128)} %bitcast.8, s32[3,24]{1,0:T(4,128)} %bitcast.9, f32[24,32]{1,0:T(8,128)} %gap.1, bf16[1,24,2,8,32]{4,3,2,1,0:T(8,128)(2,1)} %bitcast.5, bf16[1,24]{1,0:T(2,128)(2,1)} %weight.1), custom_call_target="tpu_custom_call" | custom-call | tf_op jit(solution)/shard_map/pallas_call | solution.py:292
  16.3 0.0 copy-start
  16.3 0.7 %copy-done = f32[2,24]{1,0:T(2,128)S(1)} copy-done((f32[2,24]{1,0:T(2,128)S(1)}, f32[2,24]{1,0:T(2,128)}, u32[]{:S(2)}) %copy-start) | copy-done | bytes 216
  16.9 0.6 %copy.9 = f32[24,2]{0,1:T(2,128)} copy(f32[24,2]{0,1:T(2,128)S(1)} %bitcast.7) | data formatting | bytes 384
Async XLA Ops:
  16.3 0.7 %copy-start = (f32[2,24]{1,0:T(2,128)S(1)}, f32[2,24]{1,0:T(2,128)}, u32[]{:S(2)}) copy-start(f32[2,24]{1,0:T(2,128)} %shard_map.73) | copy-start | bytes 580

commit v3 on v2

--- a/solution.py
+++ b/solution.py
@@ -26,9 +26,25 @@
         pl.loop(1, n)(f)
 
 
+def circle(turns):
+    turns = turns - NKG * jnp.floor(turns * (1.0 / NKG) + 0.5)
+    size = jnp.abs(turns)
+
+    def sine_of(x):
+        x = x * (2.0 * math.pi / NKG)
+        y = x * x
+        z = 1.0 / 6227020800.0
+        for c in (-1.0 / 39916800.0, 1.0 / 362880.0, -1.0 / 5040.0, 1.0 / 120.0, -1.0 / 6.0, 1.0):
+            z = z * y + c
+        return x * z
+
+    sine = sine_of(jnp.minimum(size, NKG // 2 - size))
+    return sine_of(NKG // 4 - size), jnp.where(turns < 0, -sine, sine)
+
+
 def kernel(
-    dims, pol, blk, coords, kidx, gap, coup, weight, out,
-    stage, gath, gpart, gall, part,
+    dims, pol_in, blk_in, coords_in, kidx_in, gap_in, coup_in, weight_in, out,
+    pol, blk, coords, kidx, gap, coup, weight, in_sem, stage, gath, gpart, gall, part,
     w_send, w_recv, g_send, g_recv, b_send, b_recv, p_send, p_recv,
 ):
     ren, kan = dims
@@ -62,7 +78,19 @@
     each(kan, hello_ka)
     each(ren, hello_re)
 
+    loads = [
+        pltpu.make_async_copy(source, to, in_sem.at[i])
+        for i, (source, to) in enumerate([
+            (blk_in, blk), (coords_in, coords), (pol_in, pol), (coup_in, coup),
+            (weight_in, weight), (kidx_in, kidx), (gap_in, gap),
+        ])
+    ]
+    for load in loads:
+        load.start()
+
     stage[...] = jnp.zeros_like(stage)
+    for load in loads[:3]:
+        load.wait()
     for r in range(own_r):
         stage[2 * r : 2 * r + 2, :] = (
             blk[r, 0].astype(F32) * pol[0] + blk[r, 1].astype(F32) * pol[1] + blk[r, 2].astype(F32) * pol[2]
@@ -76,8 +104,9 @@
     whole = stage[...]
     high = whole.astype(BF16)
     gath[ka, 0:half, :] = high
-    gath[ka, half:, :] = (whole - high.astype(F32)).astype(BF16)
-
+
+    for load in loads[3:]:
+        load.wait()
     for q in range(q_own):
         flat = jnp.concatenate(
             [coup[q, :, part_of].astype(F32).reshape(rows, nb) for part_of in range(2)], axis=1
@@ -168,25 +197,24 @@
         where = block[:, 0:half, 0:NC_LANES].astype(F32)
         here = jnp.sum(where, axis=0)[2 * own_r : 2 * own_r + 3]
         turns = kcols[0] * here[0:1] + kcols[1] * here[1:2] + kcols[2] * here[2:3]
-        turns = turns - NKG * jnp.floor(turns * (1.0 / NKG))
-        angle = turns * (2.0 * math.pi / NKG)
-        cosine = jnp.where(used, jnp.cos(angle), 0.0)
-        sine = jnp.where(used, jnp.sin(angle), 0.0)
+        cosine, sine = circle(turns)
+        cosine = jnp.where(used, cosine, 0.0)
+        sine = jnp.where(used, sine, 0.0)
         left = jnp.concatenate(
             [jnp.where(even, cosine, -sine), jnp.where(even, sine, cosine)], axis=0
         ).astype(BF16)
         return jnp.dot(
             left, block[:, 0:half].reshape(group * half, cols), preferred_element_type=F32
-        ) + jnp.dot(left, block[:, half:].reshape(group * half, cols), preferred_element_type=F32)
+        )
 
     if kan == group:
-        part[re] = partial_of(0)
+        part[re] = partial_of(0).astype(BF16)
     else:
-        part[re] = partial_of(0)
+        part[re] = partial_of(0).astype(BF16)
 
         @pl.loop(1, kan // group)
         def _(g):
-            part[re] += partial_of(g)
+            part[re] = (part[re].astype(F32) + partial_of(g)).astype(BF16)
 
     def p_copy(i):
         return pltpu.make_async_remote_copy(
@@ -205,9 +233,9 @@
         ).wait_recv()
 
     each(ren, p_wait)
-    total = part[0]
+    total = part[0].astype(F32)
     for i in range(1, ren):
-        total = total + part[i]
+        total = total + part[i].astype(F32)
     real = total[0:count] / gaps
     imag = total[count:] / gaps
     per = NC_LANES // nb
@@ -289,22 +317,7 @@
     q_out = q_own * kan // ren
     vmem = pl.BlockSpec(memory_space=pltpu.VMEM)
     dma = pltpu.SemaphoreType.DMA
-    rates = pl.pallas_call(
-        functools.partial(kernel, dims),
-        out_shape=jax.ShapeDtypeStruct((q_out, count), F32),
-        in_specs=[pl.BlockSpec(memory_space=pltpu.SMEM)] + [vmem] * 6,
-        out_specs=vmem,
-        scratch_shapes=[
-            pltpu.VMEM((half, cols), F32),
-            pltpu.VMEM((kan, 2 * half, cols), BF16),
-            pltpu.VMEM((ren, q_own * tall, NC_LANES), F32),
-            pltpu.VMEM((q_out, tall, NC_LANES), F32),
-            pltpu.VMEM((ren, 2 * count, cols), F32),
-            dma((kan,)), dma((kan,)), dma((1,)), dma((ren,)),
-            dma((kan,)), dma((q_out // q_own,)), dma((ren,)), dma((ren,)),
-        ],
-        compiler_params=pltpu.CompilerParams(collective_id=0, has_side_effects=True),
-    )(
+    args = (
         polarization,
         lattice_blocks.transpose(0, 2, 1, 3),
         lattice_coords.T,
@@ -313,6 +326,25 @@
         coupling.transpose(0, 1, 2, 4, 3),
         phonon_weight,
     )
+    rates = pl.pallas_call(
+        functools.partial(kernel, dims),
+        out_shape=pltpu.VMEM((q_out, count), F32),
+        in_specs=[pl.BlockSpec(memory_space=pl.ANY)] * len(args),
+        out_specs=vmem,
+        scratch_shapes=[pltpu.SMEM(polarization.shape, F32)]
+        + [pltpu.VMEM(x.shape, x.dtype) for x in args[1:]]
+        + [
+            dma((len(args),)),
+            pltpu.VMEM((half, cols), F32),
+            pltpu.VMEM((kan, half, cols), BF16),
+            pltpu.VMEM((ren, q_own * tall, NC_LANES), F32),
+            pltpu.VMEM((q_out, tall, NC_LANES), F32),
+            pltpu.VMEM((ren, 2 * count, cols), BF16),
+            dma((kan,)), dma((kan,)), dma((1,)), dma((ren,)),
+            dma((kan,)), dma((q_out // q_own,)), dma((ren,)), dma((ren,)),
+        ],
+        compiler_params=pltpu.CompilerParams(collective_id=0, has_side_effects=True),
+    )(*args)
     return rates.T
 
 

time: 17.6 us -> 14.3 us (0.81)
  Pallas kernels: 16.3 us -> 13.6 us
  local copies, waits for them, and re-layouts: 1.21 us -> 0.56 us
    pallas_call x1, Pallas kernels: 16.3 us -> 13.6 us  [body(): pl.pallas_call(functools.partial(kernel, dims), out_shape=pltpu.VMEM((q_o...]
    unnamed x3 -> x1, local copies, waits for them, and re-layouts: 1.21 us -> 0.56 us
where the time goes in v3:
time: 14.3 us; the launch traced here: 14.2 us
  Pallas kernels  13.6 us (95%)
  local copies, waits for them, and re-layouts  0.56 us (4%)
    pallas_call x1, Pallas kernels, body(): pl.pallas_call(functools.partial(kernel, dims), out_shape=pltpu.VMEM((q_o...  13.6 us
    unnamed x1, local copies, waits for them, and re-layouts  0.56 us

profile of v3, /device:TPU:0, one launch (start us, length us, event | category | flops | bytes accessed | tf_op | source)
XLA Modules:
  0.0 14.2 jit_solution(5057531367722779398)
XLA Ops:
  0.0 13.6 %shard_map.73 = f32[2,24]{1,0:T(2,128)S(1)} custom-call(f32[3]{0:T(128)} %pol_in.1, bf16[6,3,2,256]{3,2,1,0:T(2,128)(2,1)} %bitcast.7, s32[3,6]{1,0:T(4,128)} %bitcast.8, s32[3,24]{1,0:T(4,128)} %bitcast.9, f32[24,32]{1,0:T(8,128)} %gap_in.1, bf16[1,24,2,8,32]{4,3,2,1,0:T(8,128)(2,1)} %bitcast.6, bf16[1,24]{1,0:T(2,128)(2,1)} %weight_in.1), custom_call_target="tpu_custom_call" | custom-call | tf_op jit(solution)/shard_map/pallas_call | solution.py:329
  13.6 0.6 %copy.9 = f32[24,2]{0,1:T(2,128)} copy(f32[24,2]{0,1:T(2,128)S(1)} %bitcast.5) | data formatting | bytes 384
